TPU v7x, 32 devices: a whole 2x2x4 slice. The times are simulated.
32 devices in a mesh: trial: 4 (over y, x), dp: 4 (over z), tp: 2 (over core).
Axes of the slice: x: 2, y: 2, z: 4, core: 2. Of those that a mesh axis runs over, the one named last changes fastest.
Arguments:
- slope_query: float32 [16, 768, 768], P(('trial', 'dp'), None, 'tp'), parts along dimension 0, may hold values from -4 to 4
- slope_key: float32 [16, 768, 768], P(('trial', 'dp'), None, 'tp'), parts along dimension 0, may hold values from -4 to 4
- slope_value: float32 [16, 768, 768], P(('trial', 'dp'), None, 'tp'), parts along dimension 0, may hold values from -4 to 4
- slope_mixed: float32 [16, 768, 768], P(('trial', 'dp'), 'tp'), parts along dimension 0, may hold values from -4 to 4
- slope_norm: float32 [16, 768], P(('trial', 'dp')), parts along dimension 0, may hold values from -8 to 8
- slope_bias: float32 [16, 768], P(('trial', 'dp')), parts along dimension 0, may hold values from -8 to 8
- param_query: float32 [3072, 768], P(('trial', 'dp'), 'tp'), parts along dimension 0, may hold values from -0.3125 to 0.3125
- param_key: float32 [3072, 768], P(('trial', 'dp'), 'tp'), parts along dimension 0, may hold values from -0.3125 to 0.3125
- param_value: float32 [3072, 768], P(('trial', 'dp'), 'tp'), parts along dimension 0, may hold values from -0.3125 to 0.3125
- param_mixed: float32 [3072, 768], P(('trial', 'tp'), 'dp'), parts along dimension 0, may hold values from -0.3125 to 0.3125
- param_norm: float32 [3072], P(('trial', 'dp')), parts along dimension 0, may hold values from 0.25 to 1.75
- param_bias: float32 [3072], P(('trial', 'dp')), parts along dimension 0, may hold values from -3 to 3
- state_query: float32 [3072, 768], P(('trial', 'dp'), 'tp'), parts along dimension 0, may hold values from 0.00026041668 to 0.0026041667
- state_key: float32 [3072, 768], P(('trial', 'dp'), 'tp'), parts along dimension 0, may hold values from 0.00026041668 to 0.0026041667
- state_value: float32 [3072, 768], P(('trial', 'dp'), 'tp'), parts along dimension 0, may hold values from 0.00026041668 to 0.0026041667
- state_mixed: float32 [3072, 768], P(('trial', 'tp'), 'dp'), parts along dimension 0, may hold values from 0.00026041668 to 0.0026041667
- state_norm: float32 [3072], P(('trial', 'dp')), parts along dimension 0, may hold values from 0.05 to 0.8
- state_bias: float32 [3072], P(('trial', 'dp')), parts along dimension 0, may hold values from 0.05 to 0.8
Outputs:
- half_query: bfloat16 [3072, 768], P('trial', 'tp'), parts along dimension 0
- half_key: bfloat16 [3072, 768], P('trial', 'tp'), parts along dimension 0
- half_value: bfloat16 [3072, 768], P('trial', 'tp'), parts along dimension 0
- half_mixed: bfloat16 [3072, 768], P(('trial', 'tp')), parts along dimension 0
- half_norm: bfloat16 [3072], P('trial'), parts along dimension 0
- half_bias: bfloat16 [3072], P('trial'), parts along dimension 0
- next_query: float32 [3072, 768], P(('trial', 'dp'), 'tp'), parts along dimension 0
- next_key: float32 [3072, 768], P(('trial', 'dp'), 'tp'), parts along dimension 0
- next_value: float32 [3072, 768], P(('trial', 'dp'), 'tp'), parts along dimension 0
- next_mixed: float32 [3072, 768], P(('trial', 'tp'), 'dp'), parts along dimension 0
- next_norm: float32 [3072], P(('trial', 'dp')), parts along dimension 0
- next_bias: float32 [3072], P(('trial', 'dp')), parts along dimension 0
- state_new_query: float32 [3072, 768], P(('trial', 'dp'), 'tp'), parts along dimension 0
- state_new_key: float32 [3072, 768], P(('trial', 'dp'), 'tp'), parts along dimension 0
- state_new_value: float32 [3072, 768], P(('trial', 'dp'), 'tp'), parts along dimension 0
- state_new_mixed: float32 [3072, 768], P(('trial', 'tp'), 'dp'), parts along dimension 0
- state_new_norm: float32 [3072], P(('trial', 'dp')), parts along dimension 0
- state_new_bias: float32 [3072], P(('trial', 'dp')), parts along dimension 0
There are 4 independent parts, one for each index of `trial`. A program takes and returns all parts, laid end to end along the dimension named above; each array names one. Nothing has to cross between parts.
All inputs are finite; a program needn't handle non-finite values.
Results may differ from a plain program's by a relative error of at most 0.001.
Values may be sent and summed in bfloat16 or wider, within the bound.
A program may use at most 64 MiB of HBM per device.

v0:
```python
import functools

import jax
import jax.numpy as jnp
from jax import lax
from jax.experimental import pallas as pl
from jax.experimental.pallas import tpu as pltpu
from jax.sharding import PartitionSpec as P

learn_rate = 0.02
hold_rate = 0.8


def shards(
    slope_query,
    slope_key,
    slope_value,
    slope_mixed,
    slope_norm,
    slope_bias,
    param_query,
    param_key,
    param_value,
    param_mixed,
    param_norm,
    param_bias,
    state_query,
    state_key,
    state_value,
    state_mixed,
    state_norm,
    state_bias,
):
    mean_query, mean_key, mean_value, mean_mixed = (
        lax.psum_scatter(slope_query[0], "dp", scatter_dimension=0, tiled=True),
        lax.psum_scatter(slope_key[0], "dp", scatter_dimension=0, tiled=True),
        lax.psum_scatter(slope_value[0], "dp", scatter_dimension=0, tiled=True),
        lax.psum_scatter(slope_mixed[0], "dp", scatter_dimension=1, tiled=True),
    )
    whole_norm, whole_bias = lax.psum((slope_norm[0], slope_bias[0]), "dp")
    place = lax.axis_index("dp")
    mean_norm = lax.dynamic_slice_in_dim(
        whole_norm, place * param_norm.shape[0], param_norm.shape[0]
    )
    mean_bias = lax.dynamic_slice_in_dim(
        whole_bias, place * param_bias.shape[0], param_bias.shape[0]
    )
    mean_rate = lax.axis_size("dp") ** (-0.5)
    mean_query = mean_query * mean_rate
    mean_key = mean_key * mean_rate
    mean_value = mean_value * mean_rate
    mean_mixed = mean_mixed * mean_rate
    mean_norm = mean_norm * mean_rate
    mean_bias = mean_bias * mean_rate
    (
        own_query,
        own_key,
        own_value,
        own_mixed,
        slope_query_norm,
        slope_key_norm,
        slope_value_norm,
        slope_mixed_norm,
    ) = lax.psum(
        (
            jnp.sum(param_query * param_query, axis=1, keepdims=True),
            jnp.sum(param_key * param_key, axis=1, keepdims=True),
            jnp.sum(param_value * param_value, axis=1, keepdims=True),
            jnp.sum(param_mixed * param_mixed, axis=0, keepdims=True),
            jnp.sum(mean_query * mean_query, axis=1, keepdims=True),
            jnp.sum(mean_key * mean_key, axis=1, keepdims=True),
            jnp.sum(mean_value * mean_value, axis=1, keepdims=True),
            jnp.sum(mean_mixed * mean_mixed, axis=0, keepdims=True),
        ),
        "tp",
    )
    mean_query = mean_query * (jnp.sqrt(own_query) * lax.rsqrt(slope_query_norm + 1e-06))
    mean_key = mean_key * (jnp.sqrt(own_key) * lax.rsqrt(slope_key_norm + 1e-06))
    mean_value = mean_value * (jnp.sqrt(own_value) * lax.rsqrt(slope_value_norm + 1e-06))
    mean_mixed = mean_mixed * (jnp.sqrt(own_mixed) * lax.rsqrt(slope_mixed_norm + 1e-06))
    state_new_query = hold_rate * state_query + (1.0 - hold_rate) * mean_query * mean_query
    next_query = param_query - learn_rate * mean_query * lax.rsqrt(state_new_query + 1e-06)
    state_new_key = hold_rate * state_key + (1.0 - hold_rate) * mean_key * mean_key
    next_key = param_key - learn_rate * mean_key * lax.rsqrt(state_new_key + 1e-06)
    state_new_value = hold_rate * state_value + (1.0 - hold_rate) * mean_value * mean_value
    next_value = param_value - learn_rate * mean_value * lax.rsqrt(state_new_value + 1e-06)
    state_new_mixed = hold_rate * state_mixed + (1.0 - hold_rate) * mean_mixed * mean_mixed
    next_mixed = param_mixed - learn_rate * mean_mixed * lax.rsqrt(state_new_mixed + 1e-06)
    state_new_norm = hold_rate * state_norm + (1.0 - hold_rate) * mean_norm * mean_norm
    next_norm = param_norm - learn_rate * mean_norm * lax.rsqrt(state_new_norm + 1e-06)
    state_new_bias = hold_rate * state_bias + (1.0 - hold_rate) * mean_bias * mean_bias
    next_bias = param_bias - learn_rate * mean_bias * lax.rsqrt(state_new_bias + 1e-06)
    half_query, half_key, half_value, half_mixed, half_norm, half_bias = (
        lax.all_gather(next_query.astype(jnp.bfloat16), "dp", axis=0, tiled=True),
        lax.all_gather(next_key.astype(jnp.bfloat16), "dp", axis=0, tiled=True),
        lax.all_gather(next_value.astype(jnp.bfloat16), "dp", axis=0, tiled=True),
        lax.all_gather(next_mixed.astype(jnp.bfloat16), "dp", axis=1, tiled=True),
        lax.all_gather(next_norm.astype(jnp.bfloat16), "dp", axis=0, tiled=True),
        lax.all_gather(next_bias.astype(jnp.bfloat16), "dp", axis=0, tiled=True),
    )
    return (
        half_query,
        half_key,
        half_value,
        half_mixed,
        half_norm,
        half_bias,
        next_query,
        next_key,
        next_value,
        next_mixed,
        next_norm,
        next_bias,
        state_new_query,
        state_new_key,
        state_new_value,
        state_new_mixed,
        state_new_norm,
        state_new_bias,
    )


MESH = pl.DeviceIdType.MESH
GAIN = 1024.0
ORDER = (0, 3, 1, 2)
PIECES = 4
SENT = ((2, 0), (3, 0), (1, 1))
STEPS = ("G2", "N2", "F0", "G3", "N3", "A", "G0", "T")
LATE = {"N3": 0, "N2": 0, "F0": 2, "T": 1, "A": 2, "G2": 5, "G0": 16, "G3": 22}
END_LAG = 3


def plan_of(mesh):
    n, pair = mesh.shape["dp"], mesh.shape["tp"]
    return n if pair == 2 and n == 4 else None


def encode(x):
    t = x * GAIN
    t = t * t
    t = t * t
    t = t * t
    return jnp.where(x < 0, -t, t).astype(jnp.bfloat16)


def decode(y):
    y = y.astype(jnp.float32)
    fourth = lax.rsqrt(lax.rsqrt(jnp.abs(y)))
    root = fourth * lax.rsqrt(jnp.maximum(fourth, 1e-30)) * (1.0 / GAIN)
    return jnp.where(y < 0, -root, root)


def update(param, state, mean):
    state_new = hold_rate * state + (1.0 - hold_rate) * mean * mean
    return state_new, param - learn_rate * mean * lax.rsqrt(state_new + 1e-06)


def kernel(n, *refs):
    (sq, sk, sv, sm, sn, sb, pq, pk, pv, pm, pn, pb, tq, tk, tv, tm, tn, tb) = refs[:18]
    G, HM, hn, hb, NX, NS, xn, xb, nn, nb = refs[18:28]
    (X, XM, S, RN, RF, TOT, P_, T_, ES, ER, VS, VP, VR, VN, VO,
     load_sem, bulk_sem, par_sem, vec_sem, tx, rn_sem, rf_sem, ag_sem,
     e_send, e_recv, v_send, v_recv, vn_send, vn_recv) = refs[28:]
    H = PIECES
    own, W = X.shape[2:]
    rows = n * own
    B = own // H
    C = H * len(ORDER)
    me = lax.axis_index("dp")
    core = lax.axis_index("tp")
    rate = float(n) ** (-0.5)
    slopes, params, states = (sq, sk, sv, sm), (pq, pk, pv, pm), (tq, tk, tv, tm)
    low = me < n // 2
    end = jnp.logical_or(me == 0, me == n - 1)

    def ref(k):
        return jnp.where(low, k, n - 1 - k)

    near = jnp.where(end, ref(1), ref(0))
    far = ref(2)

    barrier = pltpu.get_barrier_semaphore()
    pl.semaphore_signal(barrier, inc=1, device_id={"dp": near}, device_id_type=MESH)

    @pl.when(jnp.logical_not(end))
    def _():
        pl.semaphore_signal(barrier, inc=1, device_id={"dp": far}, device_id_type=MESH)

    pl.semaphore_signal(barrier, inc=1, device_id={"tp": 1 - core}, device_id_type=MESH)

    def at(c):
        return c // H, pl.ds(pl.multiple_of(lax.rem(c, H) * B, 16), B)

    def load(h):
        part = pl.ds(pl.multiple_of(h * B, 16), B)
        return pltpu.make_async_copy(slopes[ORDER[0]].at[:, part], X.at[0, :, part], load_sem.at[h])

    bulk = [
        pltpu.make_async_copy(sm.at[0], XM, bulk_sem.at[k]) if m == 3
        else pltpu.make_async_copy(slopes[m], X.at[k], bulk_sem.at[k])
        for k, m in enumerate(ORDER)
        if k
    ]
    pars = [
        pltpu.make_async_copy(src[m], dst.at[k], par_sem.at[i, k])
        for k, m in enumerate(ORDER)
        for i, (src, dst) in enumerate(((params, P_), (states, T_)))
    ]
    for h in range(H):
        load(h).start()

    def vec_loads(three):
        return [
            pltpu.make_async_copy(three[0], VS, vec_sem.at[0]),
            pltpu.make_async_copy(three[1], VP.at[0], vec_sem.at[1]),
            pltpu.make_async_copy(three[2], VP.at[1], vec_sem.at[2]),
        ]

    @pl.when(core == 0)
    def _():
        for cp in vec_loads((sn, pn, tn)):
            cp.start()

    @pl.when(core == 1)
    def _():
        for cp in vec_loads((sb, pb, tb)):
            cp.start()

    for cp in bulk[:1] + pars[:2] + bulk[1:] + pars[2:]:
        cp.start()

    def remote(src, dst, ss, rs, to):
        return pltpu.make_async_remote_copy(
            src_ref=src, dst_ref=dst, send_sem=ss, recv_sem=rs, device_id={"dp": to}, device_id_type=MESH
        )

    def to_near_rs(c, j):
        m, part = at(c)
        return remote(S.at[m, j, part], RF.at[m, j, part], tx.at[0], rf_sem.at[c, j], near)

    def end_to_near_rs(c, j):
        m, part = at(c)
        return remote(S.at[m, j, part], RN.at[m, j, part], tx.at[0], rn_sem.at[c, j], near)

    def to_far_rs(c, j):
        m, part = at(c)
        return remote(S.at[m, j, part], RF.at[m, j, part], tx.at[0], rf_sem.at[c, j], far)

    def ag(c, j, k, to):
        m, part = at(c)
        return remote(G.at[m, j, part], G.at[m, j, part], tx.at[k], ag_sem.at[c, j], to)

    def pair(c):
        return pltpu.make_async_remote_copy(
            src_ref=ES.at[c], dst_ref=ER.at[c], send_sem=e_send, recv_sem=e_recv.at[c],
            device_id={"tp": 1 - core}, device_id_type=MESH,
        )

    def vec(j, k, to):
        return remote(VR.at[j], VR.at[j], v_send.at[k], v_recv.at[j], to)

    def vec_pair():
        return pltpu.make_async_remote_copy(
            src_ref=VN, dst_ref=VO, send_sem=vn_send, recv_sem=vn_recv,
            device_id={"tp": 1 - core}, device_id_type=MESH,
        )

    part_w = own

    def vec_start():
        for cp in vec_loads((sn, pn, tn)):
            cp.wait()
        for j in range(n):
            VR[me, j : j + 1, :part_w] = VS[:, j * part_w : (j + 1) * part_w]
        for k in range(2):
            VR[me, n + k : n + k + 1, :part_w] = VP[k]

    def vec_sum():
        total = VR[0, :n]
        for d in range(1, n):
            total = total + VR[d, :n]
        total = total * rate
        for d in range(n):
            state_new, nxt = update(VR[d, n : n + 1], VR[d, n + 1 : n + 2], total[d : d + 1])
            VN[d : d + 1] = nxt
            VN[n + d : n + d + 1] = state_new
        vec_pair().start()

    def vec_out():
        vec_pair().wait_recv()
        for k, (x_, s_, h_) in enumerate(((xn, nn, hn), (xb, nb, hb))):
            def take(blk, x_=x_, s_=s_, h_=h_):
                x_[...] = blk[pl.ds(me, 1), :part_w]
                s_[...] = blk[pl.ds(n + me, 1), :part_w]
                line = jnp.concatenate([blk[d : d + 1, :part_w] for d in range(n)], axis=1)
                h_[...] = jnp.concatenate(
                    [line[:, i * 128 : (i + 1) * 128] for i in range(rows // 128)], axis=0
                ).astype(jnp.bfloat16)

            @pl.when(core == k)
            def _(take=take):
                take(VN)

            @pl.when(core != k)
            def _(take=take):
                take(VO)

    def mixed_in():
        bulk[0].wait()
        for b in range(XM.shape[1] // 64):
            j, r = (b * 64) // own, (b * 64) % own
            if b % 2 == 0:
                t = XM[:, b * 64 : b * 64 + 128].T
            X[1, j, r : r + 64] = t[(b % 2) * 64 : (b % 2) * 64 + 64]

    def mixed_out(j):
        for b in range(rows // 128):
            @pl.when(j == b)
            def _(b=b):
                halves = [
                    G[1, r // own, r % own : r % own + 64].astype(jnp.float32)
                    for r in (b * 128, b * 128 + 64)
                ]
                HM[:, b * 128 : b * 128 + 128] = jnp.concatenate(halves, axis=0).T.astype(jnp.bfloat16)

    def sums(c, tot):
        m, part = at(c)
        mean = tot * rate
        TOT[m, part] = mean
        p = P_[m, part]
        lane = lax.broadcasted_iota(jnp.int32, (B, 128), 1)
        ES[c] = jnp.where(
            lane < 64, jnp.sum(p * p, axis=1, keepdims=True), jnp.sum(mean * mean, axis=1, keepdims=True)
        )
        pair(c).start()

    def apply(c):
        m, part = at(c)
        pair(c).wait_recv()
        both = ES[c] + ER[c]
        ratio = jnp.sqrt(both[:, :1]) * lax.rsqrt(both[:, 64:65] + 1e-06)
        state_new, nxt = update(P_[m, part], T_[m, part], TOT[m, part] * ratio)
        G[m, me, part] = nxt.astype(jnp.bfloat16)
        NX[m, part] = nxt
        NS[m, part] = state_new

    @pl.when(end)
    def _():
        pl.semaphore_wait(barrier, 2)

        def push(t, carry):
            for k, late in SENT:
                @pl.when(jnp.logical_and(t >= late, t < C + late))
                def _(k=k, late=late):
                    c, j = t - late, ref(k)
                    m, part = at(c)
                    S[m, j, part] = encode(X[m, j, part])
                    end_to_near_rs(c, j).start()

            return carry

        def first(t, carry):
            load(t).wait()
            return push(t, carry)

        lax.fori_loop(0, H, first, 0)
        vec_start()
        vec(me, 0, near).start()
        mixed_in()
        for cp in bulk[1:]:
            cp.wait()
        lax.fori_loop(H, C + max(late for _, late in SENT), push, 0)
        for cp in pars:
            cp.wait()

        def step(t, carry):
            @pl.when(t < C)
            def _():
                m, part = at(t)
                to_near_rs(t, me).wait_recv()
                sums(t, X[m, me, part] + decode(RF[m, me, part]))

            @pl.when(t >= END_LAG)
            def _():
                apply(t - END_LAG)
                ag(t - END_LAG, me, 0, near).start()

            return carry

        lax.fori_loop(0, C + END_LAG, step, 0)
        for k in range(1, n):
            vec(ref(k), 0, near).wait_recv()
        vec_sum()
        vec_out()

        def finish(c, carry):
            for k in range(1, n):
                ag(c, ref(k), 0, near).wait_recv()
            mixed_out(c - 2 * H)
            return carry

        lax.fori_loop(0, C, finish, 0)
        vec(me, 0, near).wait_send()

    @pl.when(jnp.logical_not(end))
    def _():
        pl.semaphore_wait(barrier, 3)
        vec_start()
        vec(me, 0, near).start()
        vec(me, 1, far).start()
        for h in range(H):
            load(h).wait()

        def pass_on(c, j, to, into_far):
            m, part = at(c)
            if into_far:
                end_to_near_rs(c, j).wait_recv()
                S[m, j, part] = encode(decode(RN[m, j, part]) + X[m, j, part])
                to_far_rs(c, j).start()
            else:
                to_far_rs(c, j).wait_recv()
                S[m, j, part] = encode(decode(RF[m, j, part]) + X[m, j, part])
                to_near_rs(c, j).start()

        def total(c):
            m, part = at(c)
            end_to_near_rs(c, me).wait_recv()
            to_far_rs(c, me).wait_recv()
            sums(c, X[m, me, part] + decode(RN[m, me, part]) + decode(RF[m, me, part]))

        def spread(c):
            apply(c)
            ag(c, me, 0, far).start()
            ag(c, me, 1, near).start()

        def relay(c, j, to):
            ag(c, j, 1, to).wait_recv()
            ag(c, j, 1, to).start()

        acts = {
            "N3": lambda c: pass_on(c, ref(3), far, True),
            "N2": lambda c: pass_on(c, ref(2), far, True),
            "F0": lambda c: pass_on(c, ref(0), near, False),
            "T": total,
            "A": spread,
            "G2": lambda c: relay(c, ref(2), near),
            "G0": lambda c: relay(c, ref(0), far),
            "G3": lambda c: relay(c, ref(3), near),
        }
        last = C + max(LATE.values())
        turn = last - rows // 128

        def step(t, carry):
            @pl.when(t == 1)
            def _():
                for cp in bulk[1:] + pars:
                    cp.wait()
                mixed_in()

            for name in STEPS:
                late = LATE[name]

                @pl.when(jnp.logical_and(t >= late, t < C + late))
                def _(name=name, late=late):
                    acts[name](t - late)

            @pl.when(t == 7)
            def _():
                vec(ref(0), 2, far).wait_recv()
                vec(ref(0), 2, far).start()
                vec(ref(2), 3, near).wait_recv()
                vec(ref(2), 3, near).start()

            @pl.when(t == 11)
            def _():
                vec(ref(3), 4, near).wait_recv()
                vec(ref(3), 4, near).start()
                vec_sum()

            @pl.when(t == 13)
            def _():
                vec_out()

            mixed_out(t - turn)
            return carry

        lax.fori_loop(0, last, step, 0)
        for k, (j, to) in enumerate(((me, near), (me, far), (ref(0), far), (ref(2), near), (ref(3), near))):
            vec(j, k, to).wait_send()
        remote(S, S, tx.at[1], rf_sem.at[0, 0], near).wait_send()

    remote(S, S, tx.at[0], rf_sem.at[0, 0], near).wait_send()
    pltpu.make_async_remote_copy(
        src_ref=ES, dst_ref=ER, send_sem=e_send, recv_sem=e_recv.at[0],
        device_id={"tp": 1 - core}, device_id_type=MESH,
    ).wait_send()
    vec_pair().wait_send()


def settle(n, *refs):
    G, HM, hn, hb, NX, NS, xn, xb, nn, nb = refs[:10]
    outs, sem = refs[10:28], refs[28]
    place = {m: k for k, m in enumerate(ORDER)}
    srcs = [G.at[place[m]] for m in range(3)] + [HM, hn, hb]
    srcs += [NX.at[place[m]] for m in range(4)] + [xn, xb]
    srcs += [NS.at[place[m]] for m in range(4)] + [nn, nb]
    copies = [pltpu.make_async_copy(s, d, sem.at[i]) for i, (s, d) in enumerate(zip(srcs, outs))]
    for cp in copies:
        cp.start()
    for cp in copies:
        cp.wait()


def fused(n, *args):
    slopes, params, states = list(args[:6]), list(args[6:12]), list(args[12:])
    own, width = params[0].shape
    rows = n * own
    H = PIECES
    if own % (H * 16) or own % 64 or width % 128 or rows % 128 or args[3].shape[1:] != (width, rows):
        return shards(*args)
    C, B = H * len(ORDER), own // H
    for i in range(3):
        slopes[i] = slopes[i].reshape(n, own, width)
    for group in (params, states):
        group[3] = group[3].T
        for i in (4, 5):
            group[i] = group[i].reshape(1, -1)
    hbm, vmem = pl.BlockSpec(memory_space=pltpu.HBM), pl.BlockSpec(memory_space=pltpu.VMEM)
    f32, bf16 = jnp.float32, jnp.bfloat16
    wide = -(-own // 128) * 128
    dma = pltpu.SemaphoreType.DMA
    four = len(ORDER)
    held = (
        [((four, n, own, width), bf16), ((width, rows), bf16)]
        + [((rows // 128, 128), bf16)] * 2
        + [((four, own, width), f32)] * 2
        + [((1, own), f32)] * 4
    )
    given = [pltpu.with_memory_space_constraint(x, pltpu.HBM) for x in slopes + params + states]
    blocks = pl.pallas_call(
        functools.partial(kernel, n),
        out_shape=[pltpu.VMEM(s, d) for s, d in held],
        in_specs=[hbm] * 18,
        out_specs=[vmem] * len(held),
        scratch_shapes=[
            pltpu.VMEM((four, n, own, width), f32),
            pltpu.VMEM((width, rows), f32),
            pltpu.VMEM((four, n, own, width), bf16),
            pltpu.VMEM((four, n, own, width), bf16),
            pltpu.VMEM((four, n, own, width), bf16),
            pltpu.VMEM((four, own, width), f32),
            pltpu.VMEM((four, own, width), f32),
            pltpu.VMEM((four, own, width), f32),
            pltpu.VMEM((C, B, 128), f32),
            pltpu.VMEM((C, B, 128), f32),
            pltpu.VMEM((1, rows), f32),
            pltpu.VMEM((2, 1, own), f32),
            pltpu.VMEM((n, 8, wide), f32),
            pltpu.VMEM((2 * n, wide), f32),
            pltpu.VMEM((2 * n, wide), f32),
            dma((H,)), dma((four,)), dma((2, four)), dma((3,)), dma((2,)), dma((C, n)), dma((C, n)), dma((C, n)),
            dma, dma((C,)), dma((5,)), dma((n,)), dma, dma,
        ],
        compiler_params=pltpu.CompilerParams(
            collective_id=0, has_side_effects=True, vmem_limit_bytes=48 * 2**20
        ),
        cost_estimate=pl.CostEstimate(flops=10**7, bytes_accessed=10**7, transcendentals=0),
    )(*given)
    S = jax.ShapeDtypeStruct
    final = (
        [S((n, own, width), bf16)] * 3 + [S((width, rows), bf16)] + [S((rows // 128, 128), bf16)] * 2
        + ([S((own, width), f32)] * 4 + [S((1, own), f32)] * 2) * 2
    )
    outs = list(
        pl.pallas_call(
            functools.partial(settle, n),
            out_shape=final,
            in_specs=[vmem] * len(held),
            out_specs=[hbm] * len(final),
            scratch_shapes=[dma((len(final),))],
            compiler_params=pltpu.CompilerParams(vmem_limit_bytes=2**20),
            cost_estimate=pl.CostEstimate(flops=10**6, bytes_accessed=10**7, transcendentals=0),
        )(*blocks)
    )
    for k in range(3):
        outs[k] = outs[k].reshape(rows, width)
    for k in (9, 15):
        outs[k] = outs[k].T
    for k in (4, 5, 10, 11, 16, 17):
        outs[k] = outs[k].reshape(-1)
    return tuple(outs)


def solution(mesh):
    in_specs = (
        P(("trial", "dp"), None, "tp"),
        P(("trial", "dp"), None, "tp"),
        P(("trial", "dp"), None, "tp"),
        P(("trial", "dp"), "tp", None),
        P(("trial", "dp"), None),
        P(("trial", "dp"), None),
        P(("trial", "dp"), "tp"),
        P(("trial", "dp"), "tp"),
        P(("trial", "dp"), "tp"),
        P(("trial", "tp"), "dp"),
        P(("trial", "dp")),
        P(("trial", "dp")),
        P(("trial", "dp"), "tp"),
        P(("trial", "dp"), "tp"),
        P(("trial", "dp"), "tp"),
        P(("trial", "tp"), "dp"),
        P(("trial", "dp")),
        P(("trial", "dp")),
    )
    out_specs = (
        P("trial", "tp"),
        P("trial", "tp"),
        P("trial", "tp"),
        P(("trial", "tp"), None),
        P("trial"),
        P("trial"),
        P(("trial", "dp"), "tp"),
        P(("trial", "dp"), "tp"),
        P(("trial", "dp"), "tp"),
        P(("trial", "tp"), "dp"),
        P(("trial", "dp")),
        P(("trial", "dp")),
        P(("trial", "dp"), "tp"),
        P(("trial", "dp"), "tp"),
        P(("trial", "dp"), "tp"),
        P(("trial", "tp"), "dp"),
        P(("trial", "dp")),
        P(("trial", "dp")),
    )
    plan = plan_of(mesh)
    body = shards if plan is None else functools.partial(fused, plan)
    return jax.shard_map(body, mesh=mesh, in_specs=in_specs, out_specs=out_specs, check_vma=False)
```

profile of v0, /device:TPU:0, one launch (start us, length us, event | category | flops | bytes accessed | tf_op | source)
XLA Modules:
  0.0 71.2 jit_solution(4771592742213848430)
XLA Ops:
  0.7 68.2 %shard_map.313 = (bf16[4,4,192,384]{3,2,1,0:T(8,128)(2,1)S(1)}, bf16[384,768]{1,0:T(8,128)(2,1)S(1)}, bf16[6,128]{1,0:T(8,128)(2,1)S(1)}, bf16[6,128]{1,0:T(8,12...) custom-call(f32[4,192,384]{2,1,0:T(8,128)} %bitcast.20, ...), custom_call_target="tpu_custom_call" | custom-call | flops 10000000 | bytes 10000000 | tf_op jit(solution)/shard_map/pallas_call | solution.py:540
  68.9 2.4 %shard_map.314 = (bf16[4,192,384]{2,1,0:T(8,128)(2,1)}, bf16[4,192,384]{2,1,0:T(8,128)(2,1)}, bf16[4,192,384]{2,1,0:T(8,128)(2,1)}, bf16[384,768]{1,0:T(8,128)(2...) custom-call(bf16[4,4,192,384]{3,2,1,0:T(8,128)(2,1)S(1)} %get-tuple-, ...), custom_call_target="tpu_custom_call" | custom-call | flops 1000000 | bytes 10000000 | tf_op jit(solution)/shard_map/pallas_call | solution.py:575
where the time goes:
time: 71.4 us; the launch traced here: 71.2 us
  Pallas kernels  70.5 us (99%)
    pallas_call x1, Pallas kernels, fused(): pl.pallas_call(functools.partial(kernel, n), out_shape=[pltpu.VMEM(s, d)...  68.2 us
    pallas_call x1, Pallas kernels, fused(): pl.pallas_call(functools.partial(settle, n), out_shape=final, in_specs=[v...  2.36 us

commit v1 on v0

--- a/solution.py
+++ b/solution.py
@@ -124,10 +124,10 @@
 GAIN = 1024.0
 ORDER = (0, 3, 1, 2)
 PIECES = 4
-SENT = ((2, 0), (3, 0), (1, 1))
-STEPS = ("G2", "N2", "F0", "G3", "N3", "A", "G0", "T")
-LATE = {"N3": 0, "N2": 0, "F0": 2, "T": 1, "A": 2, "G2": 5, "G0": 16, "G3": 22}
-END_LAG = 3
+SENT = ((2, 0), (3, 1), (1, 1))
+STEPS = ('T', 'F0', 'G0', 'N2', 'G2', 'G3', 'N3', 'A')
+LATE = {'N3': 1, 'N2': 0, 'F0': 3, 'T': 2, 'A': 2, 'G2': 4, 'G0': 17, 'G3': 21}
+END_LAG = 2
 
 
 def plan_of(mesh):
@@ -179,15 +179,6 @@
     near = jnp.where(end, ref(1), ref(0))
     far = ref(2)
 
-    barrier = pltpu.get_barrier_semaphore()
-    pl.semaphore_signal(barrier, inc=1, device_id={"dp": near}, device_id_type=MESH)
-
-    @pl.when(jnp.logical_not(end))
-    def _():
-        pl.semaphore_signal(barrier, inc=1, device_id={"dp": far}, device_id_type=MESH)
-
-    pl.semaphore_signal(barrier, inc=1, device_id={"tp": 1 - core}, device_id_type=MESH)
-
     def at(c):
         return c // H, pl.ds(pl.multiple_of(lax.rem(c, H) * B, 16), B)
 
@@ -206,7 +197,17 @@
         for k, m in enumerate(ORDER)
         for i, (src, dst) in enumerate(((params, P_), (states, T_)))
     ]
-    for h in range(H):
+    load(0).start()
+    barrier = pltpu.get_barrier_semaphore()
+    pl.semaphore_signal(barrier, inc=1, device_id={"dp": near}, device_id_type=MESH)
+
+    @pl.when(jnp.logical_not(end))
+    def _():
+        pl.semaphore_signal(barrier, inc=1, device_id={"dp": far}, device_id_type=MESH)
+
+    pl.semaphore_signal(barrier, inc=1, device_id={"tp": 1 - core}, device_id_type=MESH)
+
+    for h in range(1, H):
         load(h).start()
 
     def vec_loads(three):
@@ -344,6 +345,14 @@
         NX[m, part] = nxt
         NS[m, part] = state_new
 
+    def drain():
+        remote(S, S, tx.at[0], rf_sem.at[0, 0], near).wait_send()
+        pltpu.make_async_remote_copy(
+            src_ref=ES, dst_ref=ER, send_sem=e_send, recv_sem=e_recv.at[0],
+            device_id={"tp": 1 - core}, device_id_type=MESH,
+        ).wait_send()
+        vec_pair().wait_send()
+
     @pl.when(end)
     def _():
         pl.semaphore_wait(barrier, 2)
@@ -399,8 +408,10 @@
             mixed_out(c - 2 * H)
             return carry
 
-        lax.fori_loop(0, C, finish, 0)
+        lax.fori_loop(0, C - 1, finish, 0)
         vec(me, 0, near).wait_send()
+        drain()
+        finish(C - 1, 0)
 
     @pl.when(jnp.logical_not(end))
     def _():
@@ -451,6 +462,11 @@
         turn = last - rows // 128
 
         def step(t, carry):
+            @pl.when(t == 0)
+            def _():
+                vec(ref(2), 3, near).wait_recv()
+                vec(ref(2), 3, near).start()
+
             @pl.when(t == 1)
             def _():
                 for cp in bulk[1:] + pars:
@@ -468,8 +484,6 @@
             def _():
                 vec(ref(0), 2, far).wait_recv()
                 vec(ref(0), 2, far).start()
-                vec(ref(2), 3, near).wait_recv()
-                vec(ref(2), 3, near).start()
 
             @pl.when(t == 11)
             def _():
@@ -488,13 +502,7 @@
         for k, (j, to) in enumerate(((me, near), (me, far), (ref(0), far), (ref(2), near), (ref(3), near))):
             vec(j, k, to).wait_send()
         remote(S, S, tx.at[1], rf_sem.at[0, 0], near).wait_send()
-
-    remote(S, S, tx.at[0], rf_sem.at[0, 0], near).wait_send()
-    pltpu.make_async_remote_copy(
-        src_ref=ES, dst_ref=ER, send_sem=e_send, recv_sem=e_recv.at[0],
-        device_id={"tp": 1 - core}, device_id_type=MESH,
-    ).wait_send()
-    vec_pair().wait_send()
+        drain()
 
 
 def settle(n, *refs):
@@ -504,11 +512,11 @@
     srcs = [G.at[place[m]] for m in range(3)] + [HM, hn, hb]
     srcs += [NX.at[place[m]] for m in range(4)] + [xn, xb]
     srcs += [NS.at[place[m]] for m in range(4)] + [nn, nb]
-    copies = [pltpu.make_async_copy(s, d, sem.at[i]) for i, (s, d) in enumerate(zip(srcs, outs))]
-    for cp in copies:
-        cp.start()
-    for cp in copies:
-        cp.wait()
+    group = [0] * 4 + [3, 4] + [1] * 4 + [5, 6] + [2] * 4 + [7, 8]
+    for s, d, k in zip(srcs, outs, group):
+        pltpu.make_async_copy(s, d, sem.at[k]).start()
+    for k, whole in enumerate((G, NX, NS, hn, hb, xn, xb, nn, nb)):
+        pltpu.make_async_copy(whole, whole, sem.at[k]).wait()
 
 
 def fused(n, *args):
@@ -577,7 +585,7 @@
             out_shape=final,
             in_specs=[vmem] * len(held),
             out_specs=[hbm] * len(final),
-            scratch_shapes=[dma((len(final),))],
+            scratch_shapes=[dma((len(held) - 1,))],
             compiler_params=pltpu.CompilerParams(vmem_limit_bytes=2**20),
             cost_estimate=pl.CostEstimate(flops=10**6, bytes_accessed=10**7, transcendentals=0),
         )(*blocks)

time: 71.4 us -> 70.7 us (level)
  no operation moved by 1% of the time
where the time goes in v1:
time: 70.7 us; the launch traced here: 70.5 us
  Pallas kernels  69.9 us (99%)
    pallas_call x1, Pallas kernels, fused(): pl.pallas_call(functools.partial(kernel, n), out_shape=[pltpu.VMEM(s, d)...  67.6 us
    pallas_call x1, Pallas kernels, fused(): pl.pallas_call(functools.partial(settle, n), out_shape=final, in_specs=[v...  2.29 us

profile of v1, /device:TPU:0, one launch (start us, length us, event | category | flops | bytes accessed | tf_op | source)
XLA Modules:
  0.0 70.5 jit_solution(15731811696933839235)
XLA Ops:
  0.7 67.6 %shard_map.313 = (bf16[4,4,192,384]{3,2,1,0:T(8,128)(2,1)S(1)}, bf16[384,768]{1,0:T(8,128)(2,1)S(1)}, bf16[6,128]{1,0:T(8,128)(2,1)S(1)}, bf16[6,128]{1,0:T(8,12...) custom-call(f32[4,192,384]{2,1,0:T(8,128)} %bitcast.20, ...), custom_call_target="tpu_custom_call" | custom-call | flops 10000000 | bytes 10000000 | tf_op jit(solution)/shard_map/pallas_call | solution.py:548
  68.2 2.3 %shard_map.314 = (bf16[4,192,384]{2,1,0:T(8,128)(2,1)}, bf16[4,192,384]{2,1,0:T(8,128)(2,1)}, bf16[4,192,384]{2,1,0:T(8,128)(2,1)}, bf16[384,768]{1,0:T(8,128)(2...) custom-call(bf16[4,4,192,384]{3,2,1,0:T(8,128)(2,1)S(1)} %get-tuple-, ...), custom_call_target="tpu_custom_call" | custom-call | flops 1000000 | bytes 10000000 | tf_op jit(solution)/shard_map/pallas_call | solution.py:583
